TPU v7x, 32 devices: a whole 2x2x4 slice. The times are simulated.
32 devices in a mesh: dp: 8 (over z, y), mp: 4 (over x, core).
Axes of the slice: x: 2, y: 2, z: 4, core: 2. Of those that a mesh axis runs over, the one named last changes fastest.
Arguments:
- tokens: bfloat16 [8192, 4096], P('dp', 'mp'), may hold values from -6 to 6
- right_weight: bfloat16 [64, 64, 64], P('mp', 'dp'), may hold values from -0.75 to 0.75
- left_weight: bfloat16 [64, 64, 64], P('mp', 'dp'), may hold values from -0.75 to 0.75
- cotangent: bfloat16 [8192, 4096], P('dp', 'mp'), may hold values from -0.06591797 to 0.06591797
Outputs:
- activated: bfloat16 [8192, 4096], P('dp', 'mp')
- grad_right: float32 [64, 64, 64], P('mp', 'dp')
- grad_left: float32 [64, 64, 64], P('mp', 'dp')
All inputs are finite; a program needn't handle non-finite values.
Results may differ from a plain program's by a relative error of at most 0.0056.
Values may be sent and summed in bfloat16 or wider, within the bound.
A program may use at most 64 MiB of HBM per device.

v0:
```python
import jax
import jax.numpy as jnp
from jax import lax
from jax.sharding import PartitionSpec as P

NB = 64
BS = 64


def gelu_slope(pre):
    cdf = 0.5 * (1.0 + lax.erf(pre * 0.7071067811865476))
    density = jnp.exp(-0.5 * pre * pre) * 0.3989422804014327
    return cdf + pre * density


def shards(tokens, right_weight, left_weight, cotangent):
    tok_rows = tokens.shape[0]
    groups = lax.axis_size("mp")
    owned = NB // groups
    right_rows, left_rows = (
        lax.all_gather(right_weight, "dp", axis=1, tiled=True),
        lax.all_gather(left_weight, "dp", axis=1, tiled=True),
    )
    xs = tokens.reshape(tok_rows, owned, BS)
    inner = jnp.einsum("tik,ikm->tmi", xs, right_rows, preferred_element_type=jnp.float32)
    inner = inner.astype(jnp.bfloat16).reshape(tok_rows, BS * owned)
    left_four = left_rows.reshape(owned, groups, owned, BS)
    received = lax.all_to_all(inner, "mp", split_axis=1, concat_axis=1, tiled=True)
    rows = received.shape[0]
    mixed = received.reshape(rows, groups, owned, owned)
    pre_rows = jnp.einsum("tpmj,mpjn->tmn", mixed, left_four, preferred_element_type=jnp.float32)
    received, pre = (received, pre_rows)
    mixed = received.reshape(tok_rows, groups, owned, owned)
    activated = (
        jax.nn.gelu(pre, approximate=False).astype(jnp.bfloat16).reshape(tok_rows, owned * BS)
    )
    dpre = (cotangent.reshape(tok_rows, owned, BS).astype(jnp.float32) * gelu_slope(pre)).astype(
        jnp.bfloat16
    )
    part_left = jnp.einsum("tpmj,tmn->mpjn", mixed, dpre, preferred_element_type=jnp.float32)
    part_left = part_left.reshape(owned, NB, BS)
    dmixed = jnp.einsum("tmn,mpjn->tpmj", dpre, left_four, preferred_element_type=jnp.float32)
    dmixed = dmixed.astype(jnp.bfloat16).reshape(tok_rows, groups * owned * owned)
    dinner = lax.all_to_all(dmixed, "mp", split_axis=1, concat_axis=1, tiled=True)
    dinner = dinner.reshape(tok_rows, groups, owned, owned)
    part_right = jnp.einsum("tik,tqmi->ikqm", xs, dinner, preferred_element_type=jnp.float32)
    part_right = part_right.reshape(owned, BS, BS)
    grad_right, grad_left = (
        lax.psum_scatter(part_right, "dp", scatter_dimension=1, tiled=True),
        lax.psum_scatter(part_left, "dp", scatter_dimension=1, tiled=True),
    )
    return (activated, grad_right, grad_left)


def solution(mesh):
    return jax.shard_map(
        shards,
        mesh=mesh,
        in_specs=(P("dp", "mp"), P("mp", "dp", None), P("mp", "dp", None), P("dp", "mp")),
        out_specs=(P("dp", "mp"), P("mp", "dp", None), P("mp", "dp", None)),
        check_vma=False,
    )
```

profile of v0, /device:TPU:0, one launch (start us, length us, event | category | flops | bytes accessed | tf_op | source)
XLA Modules:
  0.0 236.4 jit_solution(14564301819312253097)
XLA Ops:
  7.2 28.6 %all_gather.6 = bf16[16,64,64]{2,1,0:T(8,128)(2,1)S(1)} all-gather(bf16[16,8,64]{2,1,0:T(8,128)(2,1)} %param.5), channel_id=1, replica_groups=mesh['dp'=8,'mp'=4] {'dp'}, dimensions={1}, use_global_device_ids=true | all-gather | bytes 147456 | tf_op jit(solution)/shard_map/all_gather | solution.py:21
  35.7 2.9 %copy.12 = bf16[1024,1024]{0,1:T(8,128)(2,1)S(1)} copy(bf16[1024,1024]{1,0:T(8,128)(2,1)} %param.4) | data formatting | bytes 4194304 | tf_op args[0]
  38.6 0.8 convert_bitcast_fusion.1
  39.3 2.5 %copy.13 = bf16[1024,64,16]{0,2,1:T(8,128)(2,1)} copy(bf16[1024,64,16]{0,1,2:T(8,128)(2,1)S(1)} %convert_bitcast_fusion.1) | data formatting | bytes 4194304 | tf_op jit(solution)/shard_map/convert_element_type | solution.py:26
  41.8 4.5 %all-to-all-start = ((bf16[1024,4,256]{0,2,1:T(8,128)(2,1)}), bf16[1024,4,256]{0,2,1:T(8,128)(2,1)}, u32[]{:S(2)}, u32[]{:S(2)}) async-start(bf16[1024,4,256]{0,2,1:T(8,128)(2,1)} %bitcast.86), calls=%async_computation | async-start | bytes 4194304 | tf_op jit(solution)/shard_map/all_to_all | solution.py:28
  46.3 0.0 copy-start.1
  46.3 4.1 %copy.15 = f32[1024,1024]{0,1:T(8,128)} copy(bf16[1024,1024]{1,0:T(8,128)(2,1)} %param.7) | data formatting | bytes 6291456 | tf_op jit(solution)/shard_map/convert_element_type | solution.py:37
  50.4 26.4 %all_gather.7 = bf16[16,64,64]{2,1,0:T(8,128)(2,1)S(1)} all-gather(bf16[16,8,64]{2,1,0:T(8,128)(2,1)S(1)} %copy-done.1), channel_id=1, replica_groups=mesh['dp'=8,'mp'=4] {'dp'}, dimensions={1}, use_global_device_ids=true | all-gather | bytes 147456 | tf_op jit(solution)/shard_map/all_gather | solution.py:22
  76.9 0.0 all-to-all-done
  76.9 13.7 %fusion.8 = (bf16[1024,16,64]{0,2,1:T(8,128)(2,1)S(1)}, bf16[1024,16,64]{0,2,1:T(8,128)(2,1)}) fusion(f32[1024,16,64]{0,2,1:T(8,128)} %bitcast.87, bf16[1024,4,16,16]{0,3,2,1:T(8,128)(2,1)} %bitcast.3, bf16[16,4,16,64]{3,2,1,0:T(8,128)(2,1)S(1)} %bitcast.89), kind=kOutput, calls=%fused_computation.10 | convolution fusion | flops 212860928 | bytes 10616832 | tf_op jit(solution)/shard_map/tpmj,mpjn->tmn/dot_general | solution.py:31
  90.5 0.7 convert_bitcast_fusion
  91.2 1.5 copy.16
  92.7 4.4 %all-to-all-start.1 = ((bf16[1024,4,256]{0,2,1:T(8,128)(2,1)}), bf16[1024,4,256]{0,2,1:T(8,128)(2,1)}, u32[]{:S(2)}, u32[]{:S(2)}) async-start(bf16[1024,4,256]{0,2,1:T(8,128)(2,1)} %bitcast.85), calls=%async_computation.1 | async-start | bytes 4194304 | tf_op jit(solution)/shard_map/all_to_all | solution.py:44
  97.2 0.0 reduce-scatter.5.cloned.1.call-start
  97.2 3.8 %fusion.23 = f32[16,4,16,64]{3,2,1,0:T(8,128)} fusion(bf16[1024,16,64]{0,2,1:T(8,128)(2,1)} %copy-done, bf16[1024,4,16,16]{0,3,2,1:T(8,128)(2,1)} %bitcast.3), kind=kOutput, calls=%fused_computation.34 | convolution fusion | flops 134217728 | bytes 4456448 | tf_op jit(solution)/shard_map/tpmj,tmn->mpjn/dot_general | solution.py:40
  101.0 0.0 reduce-scatter.5.cloned.1.call-update
  101.0 0.0 reduce-scatter.3.cloned.1.call-start
  101.1 21.9 %all-to-all-done.1 = bf16[1024,4,256]{0,2,1:T(8,128)(2,1)} async-done(((bf16[1024,4,256]{0,2,1:T(8,128)(2,1)}), bf16[1024,4,256]{0,2,1:T(8,128)(2,1)}, u32[]{:S(2)}, u32[]{:S(2)}) %all-to-all-start.1) | async-done | bytes 2097184 | tf_op jit(solution)/shard_map/all_to_all | solution.py:44
  122.9 3.1 %fusion.28 = f32[16,4,16,64]{3,2,1,0:T(8,128)S(1)} fusion(bf16[1024,16,64,1]{0,2,3,1:T(8,128)(2,1)S(1)} %bitcast.84, bf16[1024,4,16,16]{0,3,2,1:T(8,128)(2,1)} %bitcast.14), kind=kOutput, calls=%fused_computation.39 | convolution fusion | flops 134217728 | bytes 4456448 | tf_op jit(solution)/shard_map/tik,tqmi->ikqm/dot_general | solution.py:46
  126.0 1.0 copy.18
  127.0 0.0 reduce-scatter.3.cloned.1.call-update
  127.0 4.0 %copy.20 = bf16[1024,1024]{1,0:T(8,128)(2,1)} copy(bf16[1024,1024]{0,1:T(8,128)(2,1)} %bitcast.88) | data formatting | bytes 4194304
  131.0 32.4 %reduce-scatter.5.cloned.1.call-done = f32[16,8,64]{2,1,0:T(8,128)} async-done(((f32[16,64,64]{2,1,0:T(8,128)}), f32[16,8,64]{2,1,0:T(8,128)}) %reduce-scatter.5.cloned.1.call-update) | async-done | bytes 32784 | tf_op jit(solution)/shard_map/reduce_scatter | solution.py:50
  163.4 66.1 %reduce-scatter.3.cloned.1.call-done = f32[16,8,64]{2,1,0:T(8,128)} async-done(((f32[16,64,64]{2,1,0:T(8,128)}), f32[16,8,64]{2,1,0:T(8,128)}) %reduce-scatter.3.cloned.1.call-update) | async-done | bytes 32784 | tf_op jit(solution)/shard_map/reduce_scatter | solution.py:49
  (3 shorter events, 0.0 us)
Async XLA Ops:
  41.8 35.0 %all-to-all-start = ((bf16[1024,4,256]{0,2,1:T(8,128)(2,1)}), bf16[1024,4,256]{0,2,1:T(8,128)(2,1)}, u32[]{:S(2)}, u32[]{:S(2)}) async-start(bf16[1024,4,256]{0,2,1:T(8,128)(2,1)} %bitcast.86), calls=%async_computation | async-start | bytes 4194304 | tf_op jit(solution)/shard_map/all_to_all | solution.py:28
  46.3 4.1 %copy-start.1 = (bf16[16,8,64]{2,1,0:T(8,128)(2,1)S(1)}, bf16[16,8,64]{2,1,0:T(8,128)(2,1)}, u32[]{:S(2)}) copy-start(bf16[16,8,64]{2,1,0:T(8,128)(2,1)} %param.6) | copy-start | bytes 49156
  90.5 2.2 copy-start
  92.7 30.2 %all-to-all-start.1 = ((bf16[1024,4,256]{0,2,1:T(8,128)(2,1)}), bf16[1024,4,256]{0,2,1:T(8,128)(2,1)}, u32[]{:S(2)}, u32[]{:S(2)}) async-start(bf16[1024,4,256]{0,2,1:T(8,128)(2,1)} %bitcast.85), calls=%async_computation.1 | async-start | bytes 4194304 | tf_op jit(solution)/shard_map/all_to_all | solution.py:44
  97.2 66.2 %reduce-scatter.5.cloned.1.call-start = ((), (), s32[]{:S(2)}) async-start(), calls=%async_computation.5 | async-start | bytes 589824 | tf_op jit(solution)/shard_map/reduce_scatter | solution.py:50
  101.0 128.5 %reduce-scatter.3.cloned.1.call-start = ((), (), s32[]{:S(2)}) async-start(), calls=%async_computation.4 | async-start | bytes 589824 | tf_op jit(solution)/shard_map/reduce_scatter | solution.py:49
Sparse Core Ops, SparseCore 0:
  101.9 61.4 reduce-scatter.4
  167.4 62.1 reduce-scatter.2
where the time goes:
time: 237 us; the launch traced here: 236 us
  waiting for transfers between devices  120 us (51%)
  blocking collectives  55 us (23%)
  matrix products  21.9 us (9%)
  local copies, waits for them, and re-layouts  15.9 us (7%)
  between operations  14.1 us (6%)
  starting transfers between devices  8.99 us (4%)
    reduce_scatter x1, waiting for transfers between devices, shards(): lax.psum_scatter(part_right, 'dp', scatter_dimension=1, tiled=True)  66.1 us
    reduce_scatter x1, waiting for transfers between devices, shards(): lax.psum_scatter(part_left, 'dp', scatter_dimension=1, tiled=True)  32.4 us
    all_gather x1, blocking collectives, shards(): lax.all_gather(right_weight, 'dp', axis=1, tiled=True)  28.6 us
    all_gather x1, blocking collectives, shards(): lax.all_gather(left_weight, 'dp', axis=1, tiled=True)  26.4 us
    all_to_all x1, waiting for transfers between devices, shards(): lax.all_to_all(dmixed, 'mp', split_axis=1, concat_axis=1, tiled=True)  21.9 us
    dot_general x1, matrix products, shards(): jnp.einsum('tpmj,mpjn->tmn', mixed, left_four, preferred_element_type=jnp...  13.7 us
    unnamed x6, local copies, waits for them, and re-layouts  6.83 us
  transfers between devices with their start and end apart: 4, of which 3 were waited for; matrix products, arithmetic and copies ran while one was open for 7% of the time, Pallas kernels for 0%

commit v1 on v0

--- a/solution.py
+++ b/solution.py
@@ -19,7 +19,7 @@
     owned = NB // groups
     right_rows, left_rows = (
         lax.all_gather(right_weight, "dp", axis=1, tiled=True),
-        lax.all_gather(left_weight, "dp", axis=1, tiled=True),
+        jnp.concatenate(lax.all_gather(left_weight, "dp"), axis=1),
     )
     xs = tokens.reshape(tok_rows, owned, BS)
     inner = jnp.einsum("tik,ikm->tmi", xs, right_rows, preferred_element_type=jnp.float32)

time: 237 us -> 243 us (1.025)
  blocking collectives: 55 us -> 59.3 us
    all_gather x1, blocking collectives: 26.4 us -> 30.8 us  [shards(): lax.all_gather(left_weight, 'dp')]
where the time goes in v1:
time: 243 us; the launch traced here: 242 us
  waiting for transfers between devices  122 us (50%)
  blocking collectives  59.3 us (24%)
  matrix products  21.9 us (9%)
  local copies, waits for them, and re-layouts  16 us (7%)
  between operations  14.1 us (6%)
  starting transfers between devices  8.99 us (4%)
    reduce_scatter x1, waiting for transfers between devices, shards(): lax.psum_scatter(part_right, 'dp', scatter_dimension=1, tiled=True)  66.1 us
    reduce_scatter x1, waiting for transfers between devices, shards(): lax.psum_scatter(part_left, 'dp', scatter_dimension=1, tiled=True)  33.9 us
    all_gather x1, blocking collectives, shards(): lax.all_gather(left_weight, 'dp')  30.8 us
    all_gather x1, blocking collectives, shards(): lax.all_gather(right_weight, 'dp', axis=1, tiled=True)  28.6 us
    all_to_all x1, waiting for transfers between devices, shards(): lax.all_to_all(dmixed, 'mp', split_axis=1, concat_axis=1, tiled=True)  21.9 us
    dot_general x1, matrix products, shards(): jnp.einsum('tpmj,mpjn->tmn', mixed, left_four, preferred_element_type=jnp...  13.7 us
    unnamed x6, local copies, waits for them, and re-layouts  6.82 us
  transfers between devices with their start and end apart: 4, of which 3 were waited for; matrix products, arithmetic and copies ran while one was open for 7% of the time, Pallas kernels for 0%

profile of v1, /device:TPU:0, one launch (start us, length us, event | category | flops | bytes accessed | tf_op | source)
XLA Modules:
  0.0 242.3 jit_solution(14853187780677237730)
XLA Ops:
  7.2 28.6 %all_gather.9 = bf16[16,64,64]{2,1,0:T(8,128)(2,1)S(1)} all-gather(bf16[16,8,64]{2,1,0:T(8,128)(2,1)} %param.5), channel_id=1, replica_groups=mesh['dp'=8,'mp'=4] {'dp'}, dimensions={1}, use_global_device_ids=true | all-gather | bytes 147456 | tf_op jit(solution)/shard_map/all_gather | solution.py:21
  35.7 2.9 %copy.41 = bf16[1024,1024]{0,1:T(8,128)(2,1)S(1)} copy(bf16[1024,1024]{1,0:T(8,128)(2,1)} %param.4) | data formatting | bytes 4194304 | tf_op args[0]
  38.6 0.8 convert_bitcast_fusion.1
  39.3 0.0 copy-start.1
  39.4 2.5 %copy.42 = bf16[1024,64,16]{0,2,1:T(8,128)(2,1)} copy(bf16[1024,64,16]{0,1,2:T(8,128)(2,1)S(1)} %convert_bitcast_fusion.1) | data formatting | bytes 4194304 | tf_op jit(solution)/shard_map/convert_element_type | solution.py:26
  41.8 4.5 %all-to-all-start = ((bf16[1024,4,256]{0,2,1:T(8,128)(2,1)}), bf16[1024,4,256]{0,2,1:T(8,128)(2,1)}, u32[]{:S(2)}, u32[]{:S(2)}) async-start(bf16[1024,4,256]{0,2,1:T(8,128)(2,1)} %bitcast.89), calls=%async_computation | async-start | bytes 4194304 | tf_op jit(solution)/shard_map/all_to_all | solution.py:28
  46.3 30.8 %all-gather = bf16[128,8,64]{2,1,0:T(8,128)(2,1)S(1)} all-gather(bf16[16,8,64]{2,1,0:T(8,128)(2,1)S(1)} %copy-done.1), channel_id=2, replica_groups=mesh['dp'=8,'mp'=4] {'dp'}, dimensions={0}, use_global_device_ids=true | all-gather | bytes 147456 | tf_op jit(solution)/shard_map/all_gather | solution.py:22
  77.1 0.1 copy.43
  77.1 4.1 %copy.45 = f32[1024,1024]{0,1:T(8,128)} copy(bf16[1024,1024]{1,0:T(8,128)(2,1)} %param.7) | data formatting | bytes 6291456 | tf_op jit(solution)/shard_map/convert_element_type | solution.py:37
  81.3 13.7 %fusion.8 = (bf16[1024,16,64]{0,2,1:T(8,128)(2,1)S(1)}, bf16[1024,16,64]{0,2,1:T(8,128)(2,1)}) fusion(f32[1024,16,64]{0,2,1:T(8,128)} %bitcast.90, bf16[1024,4,16,16]{0,3,2,1:T(8,128)(2,1)} %bitcast.3, bf16[16,4,16,64]{3,2,1,0:T(8,128)(2,1)S(1)} %bitcast.92), kind=kOutput, calls=%fused_computation.10 | convolution fusion | flops 212860928 | bytes 10616832 | tf_op jit(solution)/shard_map/tpmj,mpjn->tmn/dot_general | solution.py:31
  95.0 0.7 convert_bitcast_fusion
  95.7 1.5 copy.46
  97.2 4.4 %all-to-all-start.1 = ((bf16[1024,4,256]{0,2,1:T(8,128)(2,1)}), bf16[1024,4,256]{0,2,1:T(8,128)(2,1)}, u32[]{:S(2)}, u32[]{:S(2)}) async-start(bf16[1024,4,256]{0,2,1:T(8,128)(2,1)} %bitcast.88), calls=%async_computation.1 | async-start | bytes 4194304 | tf_op jit(solution)/shard_map/all_to_all | solution.py:44
  101.6 0.0 reduce-scatter.5.cloned.1.call-start
  101.7 3.8 %fusion.23 = f32[16,4,16,64]{3,2,1,0:T(8,128)} fusion(bf16[1024,16,64]{0,2,1:T(8,128)(2,1)} %copy-done, bf16[1024,4,16,16]{0,3,2,1:T(8,128)(2,1)} %bitcast.3), kind=kOutput, calls=%fused_computation.34 | convolution fusion | flops 134217728 | bytes 4456448 | tf_op jit(solution)/shard_map/tpmj,tmn->mpjn/dot_general | solution.py:40
  105.4 0.0 reduce-scatter.5.cloned.1.call-update
  105.4 0.0 reduce-scatter.3.cloned.1.call-start
  105.5 21.9 %all-to-all-done.1 = bf16[1024,4,256]{0,2,1:T(8,128)(2,1)} async-done(((bf16[1024,4,256]{0,2,1:T(8,128)(2,1)}), bf16[1024,4,256]{0,2,1:T(8,128)(2,1)}, u32[]{:S(2)}, u32[]{:S(2)}) %all-to-all-start.1) | async-done | bytes 2097184 | tf_op jit(solution)/shard_map/all_to_all | solution.py:44
  127.3 3.1 %fusion.28 = f32[16,4,16,64]{3,2,1,0:T(8,128)S(1)} fusion(bf16[1024,16,64,1]{0,2,3,1:T(8,128)(2,1)S(1)} %bitcast.87, bf16[1024,4,16,16]{0,3,2,1:T(8,128)(2,1)} %bitcast.16), kind=kOutput, calls=%fused_computation.39 | convolution fusion | flops 134217728 | bytes 4456448 | tf_op jit(solution)/shard_map/tik,tqmi->ikqm/dot_general | solution.py:46
  130.4 1.0 copy.48
  131.4 0.0 reduce-scatter.3.cloned.1.call-update
  131.4 4.0 %copy.50 = bf16[1024,1024]{1,0:T(8,128)(2,1)} copy(bf16[1024,1024]{0,1:T(8,128)(2,1)} %bitcast.91) | data formatting | bytes 4194304
  135.4 33.9 %reduce-scatter.5.cloned.1.call-done = f32[16,8,64]{2,1,0:T(8,128)} async-done(((f32[16,64,64]{2,1,0:T(8,128)}), f32[16,8,64]{2,1,0:T(8,128)}) %reduce-scatter.5.cloned.1.call-update) | async-done | bytes 32784 | tf_op jit(solution)/shard_map/reduce_scatter | solution.py:50
  169.3 66.1 %reduce-scatter.3.cloned.1.call-done = f32[16,8,64]{2,1,0:T(8,128)} async-done(((f32[16,64,64]{2,1,0:T(8,128)}), f32[16,8,64]{2,1,0:T(8,128)}) %reduce-scatter.3.cloned.1.call-update) | async-done | bytes 32784 | tf_op jit(solution)/shard_map/reduce_scatter | solution.py:49
  (4 shorter events, 0.0 us)
Async XLA Ops:
  39.3 7.0 %copy-start.1 = (bf16[16,8,64]{2,1,0:T(8,128)(2,1)S(1)}, bf16[16,8,64]{2,1,0:T(8,128)(2,1)}, u32[]{:S(2)}) copy-start(bf16[16,8,64]{2,1,0:T(8,128)(2,1)} %param.6) | copy-start | bytes 49156
  41.8 39.4 %all-to-all-start = ((bf16[1024,4,256]{0,2,1:T(8,128)(2,1)}), bf16[1024,4,256]{0,2,1:T(8,128)(2,1)}, u32[]{:S(2)}, u32[]{:S(2)}) async-start(bf16[1024,4,256]{0,2,1:T(8,128)(2,1)} %bitcast.89), calls=%async_computation | async-start | bytes 4194304 | tf_op jit(solution)/shard_map/all_to_all | solution.py:28
  95.0 2.2 copy-start
  97.2 30.2 %all-to-all-start.1 = ((bf16[1024,4,256]{0,2,1:T(8,128)(2,1)}), bf16[1024,4,256]{0,2,1:T(8,128)(2,1)}, u32[]{:S(2)}, u32[]{:S(2)}) async-start(bf16[1024,4,256]{0,2,1:T(8,128)(2,1)} %bitcast.88), calls=%async_computation.1 | async-start | bytes 4194304 | tf_op jit(solution)/shard_map/all_to_all | solution.py:44
  101.6 67.7 %reduce-scatter.5.cloned.1.call-start = ((), (), s32[]{:S(2)}) async-start(), calls=%async_computation.5 | async-start | bytes 589824 | tf_op jit(solution)/shard_map/reduce_scatter | solution.py:50
  105.4 130.0 %reduce-scatter.3.cloned.1.call-start = ((), (), s32[]{:S(2)}) async-start(), calls=%async_computation.4 | async-start | bytes 589824 | tf_op jit(solution)/shard_map/reduce_scatter | solution.py:49
Sparse Core Ops, SparseCore 0:
  106.3 62.9 reduce-scatter.4
  173.2 62.1 reduce-scatter.2
